TPU v7x, 8 devices: a whole 2x2x1 slice. The times are simulated.
8 devices in a mesh: rep: 2 (over z, y), shard: 4 (over x, core).
Axes of the slice: x: 2, y: 2, z: 1, core: 2. Of those that a mesh axis runs over, the one named last changes fastest.
Arguments:
- ratings: float32 [6912, 128], P(('rep', 'shard')), parts along dimension 0
- obs_mask: int32 [6912, 128], P(('rep', 'shard')), parts along dimension 0
- step_counts: int32 [8, 4], P(('rep', 'shard')), parts along dimension 0
- user_init: float32 [6912, 128], P(('rep', 'shard')), parts along dimension 0
- item_init: float32 [256, 128], P(('rep', 'shard')), parts along dimension 0
Outputs:
- output 1: float32 [6912, 128], P(('rep', 'shard')), parts along dimension 0
- output 2: float32 [256, 128], P(('rep', 'shard')), parts along dimension 0
There are 2 independent parts. A program takes and returns all parts, laid end to end along the dimension named above; each array names one.
All inputs are finite; a program needn't handle non-finite values.
Results may differ from a plain program's by a relative error of at most 0.00147923.
Values are sent between devices in bfloat16 or wider.
A program may use at most 1 GiB of HBM per device.

v0:
```python
import math
import jax
import jax.numpy as jnp
from jax import lax
from jax.sharding import PartitionSpec as P

EPOCHS = 2


def solution(mesh):
    group_size = mesh.shape["shard"]
    row_spec = P(("rep", "shard"), None)
    shift_perm = [(source, (source - 1) % group_size) for source in range(group_size)]

    def local_run(ratings, obs_mask, step_counts, user_init, item_init):
        users_dev, rank_dim = user_init.shape
        items_dev = item_init.shape[0]
        step_size = 0.4 * math.sqrt(rank_dim) / (users_dev + rank_dim)
        decay_rate = 0.1 * items_dev / math.sqrt(rank_dim)
        dev_index = lax.axis_index("shard")
        step_row = step_counts[0]

        def sub_epoch(sweep_idx, carry_in):
            user_cur, item_cur = carry_in
            col_id = (dev_index + sweep_idx) % group_size
            rating_blk = lax.dynamic_slice_in_dim(ratings, col_id * items_dev, items_dev, axis=1)
            seen_blk = lax.dynamic_slice_in_dim(obs_mask, col_id * items_dev, items_dev, axis=1) != 0

            def grad_step(step_idx, inner_in):
                user_now, item_now = inner_in
                user_half = user_now.astype(jnp.bfloat16)
                item_half = item_now.astype(jnp.bfloat16)
                approx = jnp.einsum("ur,ir->ui", user_half, item_half, preferred_element_type=jnp.float32)
                err_half = jnp.where(seen_blk, approx - rating_blk, 0.0).astype(jnp.bfloat16)
                grad_user = jnp.einsum("ui,ir->ur", err_half, item_half, preferred_element_type=jnp.float32) + decay_rate * user_now
                grad_item = jnp.einsum("ui,ur->ir", err_half, user_half, preferred_element_type=jnp.float32) + decay_rate * item_now
                return user_now - step_size * grad_user, item_now - step_size * grad_item

            user_new, item_new = lax.fori_loop(0, step_row[col_id], grad_step, (user_cur, item_cur))
            return user_new, lax.ppermute(item_new, "shard", shift_perm)

        return lax.fori_loop(0, EPOCHS * group_size, sub_epoch, (user_init, item_init))

    return jax.shard_map(local_run, mesh=mesh, in_specs=(row_spec,) * 5, out_specs=(row_spec, row_spec), check_vma=False)
```

profile of v0, /device:TPU:1, one launch (start us, length us, event | category | flops | bytes accessed | tf_op | source)
XLA Modules:
  0.0 104.6 jit_solution(2264370521641363467)
XLA Ops:
  0.6 1.0 copy-done.4
  1.8 0.8 copy-done.5
  2.9 0.8 copy-done.1
  3.7 100.1 %while.53 = (s32[]{:T(128)}, f32[864,128]{1,0:T(8,128)S(1)}, f32[32,128]{1,0:T(8,128)S(1)}, s32[]{:T(128)}, s32[4]{0:T(128)S(1)}, /*index=5*/f32[864,128]{0,1:T(...) while((s32[]{:T(128)}, f32[864,128]{1,0:T(8,128)S(1)}, ...), condition=%wide.region_3.4_spmd, body=%wide.region_0.3_spmd.sunk | while | flops 22032404 | bytes 2630167 | solution.py:42
  3.7 0.6 dynamic_slice.37
  4.4 7.3 %while.54 = (s32[]{:T(128)}, f32[864,128]{1,0:T(8,128)S(1)}, f32[32,128]{1,0:T(8,128)S(1)}, s32[]{:T(128)}, f32[864,32]{0,1:T(8,128)S(1)}, /*index=5*/pred[864,32]{0,1:T(32,128)(4,1)S(1)}, s32[]{:T(128)}) while((s32[]{:T(128)}, f32[864,128]{1,0:T(8,128)S(1)}, f32[32,128]{1,0:T(8,128)S(1)}, s32[]{:T(128)}, f32[864,32]{0,1:T(8,128)S(1)}, ...), condition=%wide.region_2.2_spmd, body=%wide.region_1.1_spmd.sunk | while | flops 22004736 | bytes 2171981 | solution.py:39
  5.4 0.3 fusion.28
  6.7 0.3 fusion.28
  8.1 0.3 fusion.28
  9.4 0.3 fusion.28
  10.8 0.3 fusion.28
  11.8 5.3 %collective-permute-done = f32[32,128]{1,0:T(8,128)S(1)} collective-permute-done((f32[32,128]{1,0:T(8,128)S(1)}, f32[32,128]{1,0:T(8,128)S(1)}, u32[]{:S(2)}, u32[]{:S(2)}) %collective-permute-start) | collective-permute-done | bytes 16416 | tf_op jit(solution)/shard_map/while/body/eval_jaxpr/ppermute | solution.py:40
  17.2 0.6 dynamic_slice.37
  17.8 8.7 %while.54 = (s32[]{:T(128)}, f32[864,128]{1,0:T(8,128)S(1)}, f32[32,128]{1,0:T(8,128)S(1)}, s32[]{:T(128)}, f32[864,32]{0,1:T(8,128)S(1)}, /*index=5*/pred[864,32]{0,1:T(32,128)(4,1)S(1)}, s32[]{:T(128)}) while((s32[]{:T(128)}, f32[864,128]{1,0:T(8,128)S(1)}, f32[32,128]{1,0:T(8,128)S(1)}, s32[]{:T(128)}, f32[864,32]{0,1:T(8,128)S(1)}, ...), condition=%wide.region_2.2_spmd, body=%wide.region_1.1_spmd.sunk | while | flops 22004736 | bytes 2171981 | solution.py:39
  18.8 0.3 fusion.28
  20.2 0.3 fusion.28
  21.5 0.3 fusion.28
  22.8 0.3 fusion.28
  24.2 0.3 fusion.28
  25.5 0.3 fusion.28
  26.5 3.2 %collective-permute-done = f32[32,128]{1,0:T(8,128)S(1)} collective-permute-done((f32[32,128]{1,0:T(8,128)S(1)}, f32[32,128]{1,0:T(8,128)S(1)}, u32[]{:S(2)}, u32[]{:S(2)}) %collective-permute-start) | collective-permute-done | bytes 16416 | tf_op jit(solution)/shard_map/while/body/eval_jaxpr/ppermute | solution.py:40
  29.7 0.6 dynamic_slice.37
  30.4 8.7 %while.54 = (s32[]{:T(128)}, f32[864,128]{1,0:T(8,128)S(1)}, f32[32,128]{1,0:T(8,128)S(1)}, s32[]{:T(128)}, f32[864,32]{0,1:T(8,128)S(1)}, /*index=5*/pred[864,32]{0,1:T(32,128)(4,1)S(1)}, s32[]{:T(128)}) while((s32[]{:T(128)}, f32[864,128]{1,0:T(8,128)S(1)}, f32[32,128]{1,0:T(8,128)S(1)}, s32[]{:T(128)}, f32[864,32]{0,1:T(8,128)S(1)}, ...), condition=%wide.region_2.2_spmd, body=%wide.region_1.1_spmd.sunk | while | flops 22004736 | bytes 2171981 | solution.py:39
  31.4 0.3 fusion.28
  32.7 0.3 fusion.28
  34.1 0.3 fusion.28
  35.4 0.3 fusion.28
  36.8 0.3 fusion.28
  38.1 0.3 fusion.28
  39.1 3.2 %collective-permute-done = f32[32,128]{1,0:T(8,128)S(1)} collective-permute-done((f32[32,128]{1,0:T(8,128)S(1)}, f32[32,128]{1,0:T(8,128)S(1)}, u32[]{:S(2)}, u32[]{:S(2)}) %collective-permute-start) | collective-permute-done | bytes 16416 | tf_op jit(solution)/shard_map/while/body/eval_jaxpr/ppermute | solution.py:40
  42.3 0.6 dynamic_slice.37
  42.9 8.7 %while.54 = (s32[]{:T(128)}, f32[864,128]{1,0:T(8,128)S(1)}, f32[32,128]{1,0:T(8,128)S(1)}, s32[]{:T(128)}, f32[864,32]{0,1:T(8,128)S(1)}, /*index=5*/pred[864,32]{0,1:T(32,128)(4,1)S(1)}, s32[]{:T(128)}) while((s32[]{:T(128)}, f32[864,128]{1,0:T(8,128)S(1)}, f32[32,128]{1,0:T(8,128)S(1)}, s32[]{:T(128)}, f32[864,32]{0,1:T(8,128)S(1)}, ...), condition=%wide.region_2.2_spmd, body=%wide.region_1.1_spmd.sunk | while | flops 22004736 | bytes 2171981 | solution.py:39
  44.0 0.3 fusion.28
  48.0 0.3 fusion.28
  49.3 0.3 fusion.28
  50.7 0.3 fusion.28
  51.7 3.2 %collective-permute-done = f32[32,128]{1,0:T(8,128)S(1)} collective-permute-done((f32[32,128]{1,0:T(8,128)S(1)}, f32[32,128]{1,0:T(8,128)S(1)}, u32[]{:S(2)}, u32[]{:S(2)}) %collective-permute-start) | collective-permute-done | bytes 16416 | tf_op jit(solution)/shard_map/while/body/eval_jaxpr/ppermute | solution.py:40
  54.9 0.6 dynamic_slice.37
  55.5 7.3 %while.54 = (s32[]{:T(128)}, f32[864,128]{1,0:T(8,128)S(1)}, f32[32,128]{1,0:T(8,128)S(1)}, s32[]{:T(128)}, f32[864,32]{0,1:T(8,128)S(1)}, /*index=5*/pred[864,32]{0,1:T(32,128)(4,1)S(1)}, s32[]{:T(128)}) while((s32[]{:T(128)}, f32[864,128]{1,0:T(8,128)S(1)}, f32[32,128]{1,0:T(8,128)S(1)}, s32[]{:T(128)}, f32[864,32]{0,1:T(8,128)S(1)}, ...), condition=%wide.region_2.2_spmd, body=%wide.region_1.1_spmd.sunk | while | flops 22004736 | bytes 2171981 | solution.py:39
  57.9 0.3 fusion.28
  59.2 0.3 fusion.28
  62.9 3.2 %collective-permute-done = f32[32,128]{1,0:T(8,128)S(1)} collective-permute-done((f32[32,128]{1,0:T(8,128)S(1)}, f32[32,128]{1,0:T(8,128)S(1)}, u32[]{:S(2)}, u32[]{:S(2)}) %collective-permute-start) | collective-permute-done | bytes 16416 | tf_op jit(solution)/shard_map/while/body/eval_jaxpr/ppermute | solution.py:40
  66.1 0.6 dynamic_slice.37
  66.8 8.7 %while.54 = (s32[]{:T(128)}, f32[864,128]{1,0:T(8,128)S(1)}, f32[32,128]{1,0:T(8,128)S(1)}, s32[]{:T(128)}, f32[864,32]{0,1:T(8,128)S(1)}, /*index=5*/pred[864,32]{0,1:T(32,128)(4,1)S(1)}, s32[]{:T(128)}) while((s32[]{:T(128)}, f32[864,128]{1,0:T(8,128)S(1)}, f32[32,128]{1,0:T(8,128)S(1)}, s32[]{:T(128)}, f32[864,32]{0,1:T(8,128)S(1)}, ...), condition=%wide.region_2.2_spmd, body=%wide.region_1.1_spmd.sunk | while | flops 22004736 | bytes 2171981 | solution.py:39
  69.1 0.3 fusion.28
  70.5 0.3 fusion.28
  71.8 0.3 fusion.28
  73.1 0.3 fusion.28
  74.5 0.3 fusion.28
  75.5 3.2 %collective-permute-done = f32[32,128]{1,0:T(8,128)S(1)} collective-permute-done((f32[32,128]{1,0:T(8,128)S(1)}, f32[32,128]{1,0:T(8,128)S(1)}, u32[]{:S(2)}, u32[]{:S(2)}) %collective-permute-start) | collective-permute-done | bytes 16416 | tf_op jit(solution)/shard_map/while/body/eval_jaxpr/ppermute | solution.py:40
  78.7 0.6 dynamic_slice.37
  79.3 8.7 %while.54 = (s32[]{:T(128)}, f32[864,128]{1,0:T(8,128)S(1)}, f32[32,128]{1,0:T(8,128)S(1)}, s32[]{:T(128)}, f32[864,32]{0,1:T(8,128)S(1)}, /*index=5*/pred[864,32]{0,1:T(32,128)(4,1)S(1)}, s32[]{:T(128)}) while((s32[]{:T(128)}, f32[864,128]{1,0:T(8,128)S(1)}, f32[32,128]{1,0:T(8,128)S(1)}, s32[]{:T(128)}, f32[864,32]{0,1:T(8,128)S(1)}, ...), condition=%wide.region_2.2_spmd, body=%wide.region_1.1_spmd.sunk | while | flops 22004736 | bytes 2171981 | solution.py:39
  80.3 0.3 fusion.28
  81.7 0.3 fusion.28
  84.4 0.3 fusion.28
  85.7 0.3 fusion.28
  88.1 3.2 %collective-permute-done = f32[32,128]{1,0:T(8,128)S(1)} collective-permute-done((f32[32,128]{1,0:T(8,128)S(1)}, f32[32,128]{1,0:T(8,128)S(1)}, u32[]{:S(2)}, u32[]{:S(2)}) %collective-permute-start) | collective-permute-done | bytes 16416 | tf_op jit(solution)/shard_map/while/body/eval_jaxpr/ppermute | solution.py:40
  91.3 0.6 dynamic_slice.37
  91.9 8.7 %while.54 = (s32[]{:T(128)}, f32[864,128]{1,0:T(8,128)S(1)}, f32[32,128]{1,0:T(8,128)S(1)}, s32[]{:T(128)}, f32[864,32]{0,1:T(8,128)S(1)}, /*index=5*/pred[864,32]{0,1:T(32,128)(4,1)S(1)}, s32[]{:T(128)}) while((s32[]{:T(128)}, f32[864,128]{1,0:T(8,128)S(1)}, f32[32,128]{1,0:T(8,128)S(1)}, s32[]{:T(128)}, f32[864,32]{0,1:T(8,128)S(1)}, ...), condition=%wide.region_2.2_spmd, body=%wide.region_1.1_spmd.sunk | while | flops 22004736 | bytes 2171981 | solution.py:39
  92.9 0.3 fusion.28
  94.3 0.3 fusion.28
  95.6 0.3 fusion.28
  100.6 3.2 %collective-permute-done = f32[32,128]{1,0:T(8,128)S(1)} collective-permute-done((f32[32,128]{1,0:T(8,128)S(1)}, f32[32,128]{1,0:T(8,128)S(1)}, u32[]{:S(2)}, u32[]{:S(2)}) %collective-permute-start) | collective-permute-done | bytes 16416 | tf_op jit(solution)/shard_map/while/body/eval_jaxpr/ppermute | solution.py:40
  103.8 0.8 copy-done
  (193 shorter events, 21.2 us)
Async XLA Ops:
  0.6 1.0 copy-start.4
  1.6 1.0 copy-start.5
  2.7 1.0 copy-start.1
  2.7 1.0 copy-start.3
  2.7 1.0 copy-start.6
  11.7 5.4 %collective-permute-start = (f32[32,128]{1,0:T(8,128)S(1)}, f32[32,128]{1,0:T(8,128)S(1)}, u32[]{:S(2)}, u32[]{:S(2)}) collective-permute-start(f32[32,128]{1,0:T(8,128)S(1)} %get-tuple-element.344), channel_id=1, source_target_pairs={{0,3},{1,0},{2,1},{3,2},{4,7},{5,4},{6,5},{7,6}} | collective-permute-start | bytes 49160 | tf_op jit(solution)/shard_map/while/body/eval_jaxpr/ppermute | solution.py:40
  26.5 3.2 %collective-permute-start = (f32[32,128]{1,0:T(8,128)S(1)}, f32[32,128]{1,0:T(8,128)S(1)}, u32[]{:S(2)}, u32[]{:S(2)}) collective-permute-start(f32[32,128]{1,0:T(8,128)S(1)} %get-tuple-element.344), channel_id=1, source_target_pairs={{0,3},{1,0},{2,1},{3,2},{4,7},{5,4},{6,5},{7,6}} | collective-permute-start | bytes 49160 | tf_op jit(solution)/shard_map/while/body/eval_jaxpr/ppermute | solution.py:40
  39.1 3.2 %collective-permute-start = (f32[32,128]{1,0:T(8,128)S(1)}, f32[32,128]{1,0:T(8,128)S(1)}, u32[]{:S(2)}, u32[]{:S(2)}) collective-permute-start(f32[32,128]{1,0:T(8,128)S(1)} %get-tuple-element.344), channel_id=1, source_target_pairs={{0,3},{1,0},{2,1},{3,2},{4,7},{5,4},{6,5},{7,6}} | collective-permute-start | bytes 49160 | tf_op jit(solution)/shard_map/while/body/eval_jaxpr/ppermute | solution.py:40
  51.6 3.2 %collective-permute-start = (f32[32,128]{1,0:T(8,128)S(1)}, f32[32,128]{1,0:T(8,128)S(1)}, u32[]{:S(2)}, u32[]{:S(2)}) collective-permute-start(f32[32,128]{1,0:T(8,128)S(1)} %get-tuple-element.344), channel_id=1, source_target_pairs={{0,3},{1,0},{2,1},{3,2},{4,7},{5,4},{6,5},{7,6}} | collective-permute-start | bytes 49160 | tf_op jit(solution)/shard_map/while/body/eval_jaxpr/ppermute | solution.py:40
  62.9 3.2 %collective-permute-start = (f32[32,128]{1,0:T(8,128)S(1)}, f32[32,128]{1,0:T(8,128)S(1)}, u32[]{:S(2)}, u32[]{:S(2)}) collective-permute-start(f32[32,128]{1,0:T(8,128)S(1)} %get-tuple-element.344), channel_id=1, source_target_pairs={{0,3},{1,0},{2,1},{3,2},{4,7},{5,4},{6,5},{7,6}} | collective-permute-start | bytes 49160 | tf_op jit(solution)/shard_map/while/body/eval_jaxpr/ppermute | solution.py:40
  75.5 3.2 %collective-permute-start = (f32[32,128]{1,0:T(8,128)S(1)}, f32[32,128]{1,0:T(8,128)S(1)}, u32[]{:S(2)}, u32[]{:S(2)}) collective-permute-start(f32[32,128]{1,0:T(8,128)S(1)} %get-tuple-element.344), channel_id=1, source_target_pairs={{0,3},{1,0},{2,1},{3,2},{4,7},{5,4},{6,5},{7,6}} | collective-permute-start | bytes 49160 | tf_op jit(solution)/shard_map/while/body/eval_jaxpr/ppermute | solution.py:40
  88.0 3.2 %collective-permute-start = (f32[32,128]{1,0:T(8,128)S(1)}, f32[32,128]{1,0:T(8,128)S(1)}, u32[]{:S(2)}, u32[]{:S(2)}) collective-permute-start(f32[32,128]{1,0:T(8,128)S(1)} %get-tuple-element.344), channel_id=1, source_target_pairs={{0,3},{1,0},{2,1},{3,2},{4,7},{5,4},{6,5},{7,6}} | collective-permute-start | bytes 49160 | tf_op jit(solution)/shard_map/while/body/eval_jaxpr/ppermute | solution.py:40
  100.6 3.2 %collective-permute-start = (f32[32,128]{1,0:T(8,128)S(1)}, f32[32,128]{1,0:T(8,128)S(1)}, u32[]{:S(2)}, u32[]{:S(2)}) collective-permute-start(f32[32,128]{1,0:T(8,128)S(1)} %get-tuple-element.344), channel_id=1, source_target_pairs={{0,3},{1,0},{2,1},{3,2},{4,7},{5,4},{6,5},{7,6}} | collective-permute-start | bytes 49160 | tf_op jit(solution)/shard_map/while/body/eval_jaxpr/ppermute | solution.py:40
  103.8 0.8 copy-start
  103.8 0.8 copy-start.2
where the time goes:
time: 105 us
  loops' own time  35.8 us (34%)
  matrix products  31.1 us (30%)
  waiting for transfers between devices  27.4 us (26%)
  local copies, waits for them, and re-layouts  9.19 us (9%)
    another operation x8, loops' own time, sub_epoch(): lax.fori_loop(0, step_row[col_id], grad_step, (user_cur, item_cur))  35.6 us
    ppermute x8, waiting for transfers between devices, sub_epoch(): return (user_new, lax.ppermute(item_new, 'shard', shift_perm))  27.4 us
    dot_general x46, matrix products, grad_step(): jnp.einsum('ui,ir->ur', err_half, item_half, preferred_element_type=jnp.f...  14.4 us
    dot_general x46, matrix products, grad_step(): jnp.einsum('ur,ir->ui', user_half, item_half, preferred_element_type=jnp....  9.07 us
    dot_general x46, matrix products, grad_step(): jnp.einsum('ui,ur->ir', err_half, user_half, preferred_element_type=jnp.f...  7.63 us
    dynamic_slice x8, local copies, waits for them, and re-layouts, sub_epoch(): step_row[col_id]  5.1 us
    unnamed x14, local copies, waits for them, and re-layouts  3.4 us
  transfers between devices with their start and end apart: 8, of which 8 were waited for; matrix products, arithmetic and copies ran while one was open for 0% of the time, Pallas kernels for 0%

commit v1 on v0

v1 whole, which is shorter than its diff:
```python
import math
import jax
import jax.numpy as jnp
from jax import lax
from jax.sharding import PartitionSpec as P
from jax.experimental import pallas as pl
from jax.experimental.pallas import tpu as pltpu

EPOCHS = 2
STEPS_MAX = 6
MESH = pl.DeviceIdType.MESH
PIECE = 32


def solution(mesh):
    group_size = mesh.shape["shard"]
    row_spec = P(("rep", "shard"), None)
    sweeps = EPOCHS * group_size
    half = jnp.bfloat16

    def local_run(ratings, obs_mask, step_counts, user_init, item_init):
        users_dev, rank_dim = user_init.shape
        items_dev = item_init.shape[0]
        step_size = 0.4 * math.sqrt(rank_dim) / (users_dev + rank_dim)
        decay_rate = 0.1 * items_dev / math.sqrt(rank_dim)
        shrink = 1.0 - step_size * decay_rate
        blocks = -(-users_dev // 128)
        last_rows = users_dev - 128 * (blocks - 1)

        def place(block):
            return block // 4, (block // 2) % 2, block % 2

        def rows_of(ref, block):
            if block < blocks - 1 or last_rows == 128:
                return ref[pl.ds(128 * block, 128), :]
            tail = ref[pl.ds(128 * block, last_rows), :]
            return jnp.concatenate([tail, jnp.zeros((128 - last_rows, tail.shape[1]), tail.dtype)], axis=0)

        def sweep_kernel(counts, rating_hbm, mask_hbm, user_hbm, item_hbm, ut_out, item_out,
                         rating_in, mask_in, user_in, item_in, rt, mt, ut, uth, item_sent, load_sem, send_sem, recv_sem):
            me = lax.axis_index("shard")
            left = lax.rem(me + group_size - 1, group_size)
            right = lax.rem(me + 1, group_size)
            loads = [
                pltpu.make_async_copy(user_hbm, user_in, load_sem.at[0]),
                pltpu.make_async_copy(rating_hbm, rating_in, load_sem.at[1]),
                pltpu.make_async_copy(mask_hbm, mask_in, load_sem.at[2]),
                pltpu.make_async_copy(item_hbm, item_in.at[0], load_sem.at[3]),
            ]
            for load in loads:
                load.start()
            barrier = pltpu.get_barrier_semaphore()
            for neighbour in (left, right):
                pl.semaphore_signal(barrier, inc=1, device_id={"shard": neighbour}, device_id_type=MESH)

            loads[0].wait()
            ut[...] = jnp.zeros_like(ut)
            uth[...] = jnp.zeros_like(uth)
            rt[...] = jnp.zeros_like(rt)
            mt[...] = jnp.zeros_like(mt)
            for b in range(blocks):
                m, h, s = place(b)
                blk = rows_of(user_in, b).T
                ut[m, pl.ds(128 * h, 128), pl.ds(128 * s, 128)] = blk
                uth[m, pl.ds(128 * h, 128), pl.ds(128 * s, 128)] = blk.astype(half)
            loads[1].wait()
            for b in range(blocks):
                m, h, s = place(b)
                blk = rows_of(rating_in, b).T
                for j in range(group_size):
                    rt[m, j, pl.ds(items_dev * h, items_dev), pl.ds(128 * s, 128)] = blk[items_dev * j:items_dev * (j + 1)]
            loads[2].wait()
            for b in range(blocks):
                m, h, s = place(b)
                blk = rows_of(mask_in, b).T
                for j in range(group_size):
                    mt[m, j, pl.ds(items_dev * h, items_dev), pl.ds(128 * s, 128)] = blk[items_dev * j:items_dev * (j + 1)]
            loads[3].wait()
            pl.semaphore_wait(barrier, 2)

            lane = lax.broadcasted_iota(jnp.int32, (128, 128), 1)
            pair = 2 * items_dev

            def one_step(item_now, col, active):
                threshold = jnp.where(active, 0, 1)
                keep = jnp.where(active, jnp.float32(shrink), jnp.float32(1.0))
                item_half = item_now.astype(half)
                none = jnp.zeros_like(item_half)
                lhs_a = jnp.concatenate([
                    jnp.concatenate([item_half, none], axis=1),
                    jnp.concatenate([none, item_half], axis=1)], axis=0)
                item_t = jnp.concatenate(
                    [item_now, item_now, jnp.zeros((128 - pair, rank_dim), jnp.float32)], axis=0).T
                top = jnp.where(lane < items_dev, item_t, 0.0).astype(half)
                low = jnp.where((lane >= items_dev) & (lane < pair), item_t, 0.0).astype(half)
                lhs_u = jnp.concatenate([top, low], axis=0)[:, :pair]
                errs = []
                for m in range(2):
                    approx = jnp.dot(lhs_a, uth[m], preferred_element_type=jnp.float32)
                    seen = mt[m, col] > threshold
                    errs.append(jnp.where(seen, approx - rt[m, col], 0.0).astype(half))
                grads = [lax.dot_general(errs[m], uth[m], (((1,), (1,)), ((), ())), preferred_element_type=jnp.float32) for m in range(2)]
                grad_item = ((grads[0][:items_dev, :128] + grads[0][items_dev:, 128:])
                             + (grads[1][:items_dev, :128] + grads[1][items_dev:, 128:]))
                item_new = keep * item_now - step_size * grad_item
                for m in range(2):
                    grad = jnp.dot(lhs_u, errs[m], preferred_element_type=jnp.float32)
                    fresh = keep * ut[m] - step_size * grad
                    ut[m] = fresh
                    uth[m] = fresh.astype(half)
                return item_new

            def sub_epoch(t, carry):
                col = lax.rem(me + t, group_size)
                count = counts[0, col]
                item_now = item_in[t]
                for k in range(STEPS_MAX):
                    item_now = one_step(item_now, col, k < count)
                item_sent[t] = item_now
                hop = pltpu.make_async_remote_copy(
                    src_ref=item_sent.at[t], dst_ref=item_in.at[t + 1],
                    send_sem=send_sem.at[t], recv_sem=recv_sem.at[t],
                    device_id={"shard": left}, device_id_type=MESH)
                hop.start()
                hop.wait()
                return carry

            lax.fori_loop(0, sweeps, sub_epoch, 0)
            ut_out[...] = ut[...]
            item_out[...] = item_in[sweeps]

        vmem = pl.BlockSpec(memory_space=pltpu.VMEM)
        ut_fin, item_fin = pl.pallas_call(
            sweep_kernel,
            out_shape=(jax.ShapeDtypeStruct((2, 256, 256), jnp.float32), jax.ShapeDtypeStruct(item_init.shape, jnp.float32)),
            in_specs=[pl.BlockSpec(memory_space=pltpu.SMEM)] + [pl.BlockSpec(memory_space=pl.ANY)] * 4,
            out_specs=(vmem, vmem),
            scratch_shapes=[
                pltpu.VMEM(ratings.shape, jnp.float32),
                pltpu.VMEM(obs_mask.shape, jnp.int32),
                pltpu.VMEM(user_init.shape, jnp.float32),
                pltpu.VMEM((sweeps + 1,) + item_init.shape, jnp.float32),
                pltpu.VMEM((2, group_size, 2 * items_dev, 256), jnp.float32),
                pltpu.VMEM((2, group_size, 2 * items_dev, 256), jnp.int32),
                pltpu.VMEM((2, 256, 256), jnp.float32),
                pltpu.VMEM((2, 256, 256), half),
                pltpu.VMEM((sweeps,) + item_init.shape, jnp.float32),
                pltpu.SemaphoreType.DMA((4,)),
                pltpu.SemaphoreType.DMA((sweeps,)),
                pltpu.SemaphoreType.DMA((sweeps,)),
            ],
            compiler_params=pltpu.CompilerParams(collective_id=0, has_side_effects=True),
            name="sweeps",
        )(step_counts, ratings, obs_mask, user_init, item_init)

        def finish_kernel(ut_ref, item_ref, user_out, item_out):
            for b in range(blocks):
                m, h, s = place(b)
                blk = ut_ref[m, pl.ds(128 * h, 128), pl.ds(128 * s, 128)].T
                rows = min(128, users_dev - 128 * b)
                user_out[pl.ds(128 * b, rows), :] = blk[:rows]
            item_out[...] = item_ref[...]

        return pl.pallas_call(
            finish_kernel,
            out_shape=(jax.ShapeDtypeStruct(user_init.shape, jnp.float32), jax.ShapeDtypeStruct(item_init.shape, jnp.float32)),
            in_specs=[vmem, vmem],
            out_specs=(vmem, vmem),
            name="finish",
        )(ut_fin, item_fin)

    return jax.shard_map(local_run, mesh=mesh, in_specs=(row_spec,) * 5, out_specs=(row_spec, row_spec), check_vma=False)
```

time: 105 us -> 37.9 us (0.36)
  the two profiles are of different devices: /device:TPU:1 before, /device:TPU:0 now
where the time goes in v1:
time: 37.9 us; the launch traced here: 37.7 us
  Pallas kernels  37.1 us (98%)
  between operations  0.64 us (2%)
    pallas_call x1, Pallas kernels, local_run(): pl.pallas_call(sweep_kernel, out_shape=(jax.ShapeDtypeStruct((2, 256, 256...  35.1 us
    pallas_call x1, Pallas kernels, local_run(): pl.pallas_call(finish_kernel, out_shape=(jax.ShapeDtypeStruct(user_init.s...  2 us

profile of v1, /device:TPU:0, one launch (start us, length us, event | category | flops | bytes accessed | tf_op | source)
XLA Modules:
  0.0 37.7 jit_solution(2460917521971398911)
XLA Ops:
  0.6 35.1 %sweeps.1 = (f32[2,256,256]{2,1,0:T(8,128)}, f32[32,128]{1,0:T(8,128)}) custom-call(s32[1,4]{1,0:T(1,128)} %counts.1, f32[864,128]{1,0:T(8,128)} %rating_hbm.1, s32[864,128]{1,0:T(8,128)} %mask_hbm.1, f32[864,128]{1,0:T(8,128)} %user_hbm.1, f32[32,128]{1,0:T(8,128)} %item_hbm.1), custom_call_target="tpu_custom_call" | custom-call | tf_op jit(solution)/shard_map/sweeps/pallas_call | solution.py:133
  35.7 2.0 %finish.1 = (f32[864,128]{1,0:T(8,128)}, f32[32,128]{1,0:T(8,128)}) custom-call(f32[2,256,256]{2,1,0:T(8,128)} %get-tuple-element.4.ut_ref, f32[32,128]{1,0:T(8,128)} %get-tuple-element.5.item_ref), custom_call_target="tpu_custom_call" | custom-call | tf_op jit(solution)/shard_map/finish/pallas_call | solution.py:164

commit v2 on v0

v2 whole, which is shorter than its diff:
```python
import math
import jax
import jax.numpy as jnp
from jax import lax
from jax.sharding import PartitionSpec as P
from jax.experimental import pallas as pl
from jax.experimental.pallas import tpu as pltpu

EPOCHS = 2
STEPS_MAX = 6
MESH = pl.DeviceIdType.MESH
LANES = 128
GROUP = 256


def solution(mesh):
    group_size = mesh.shape["shard"]
    row_spec = P(("rep", "shard"), None)
    sweeps = EPOCHS * group_size
    half = jnp.bfloat16
    full = jnp.float32

    def local_run(ratings, obs_mask, step_counts, user_init, item_init):
        users_dev, rank_dim = user_init.shape
        items_dev = item_init.shape[0]
        step_size = 0.4 * math.sqrt(rank_dim) / (users_dev + rank_dim)
        decay_rate = 0.1 * items_dev / math.sqrt(rank_dim)
        shrink = 1.0 - step_size * decay_rate
        blocks = -(-users_dev // LANES)
        groups = -(-users_dev // GROUP)
        biggest = float(jnp.finfo(full).max)

        def rows_of(ref, block):
            rows = min(LANES, users_dev - LANES * block)
            part = ref[pl.ds(LANES * block, rows), :]
            if rows == LANES:
                return part
            return jnp.concatenate([part, jnp.zeros((LANES - rows, part.shape[1]), part.dtype)], axis=0)

        def sweep_kernel(counts_hbm, rating_hbm, mask_hbm, user_hbm, item_hbm, user_out, item_out,
                         counts, rating_in, mask_in, user_in, item_in, item_sent, rt, ut, uth, load_sem, send_sem, recv_sem):
            me = lax.axis_index("shard")
            left = lax.rem(me + group_size - 1, group_size)
            right = lax.rem(me + 1, group_size)
            load_user = pltpu.make_async_copy(user_hbm, user_in, load_sem.at[0])
            load_rating = pltpu.make_async_copy(rating_hbm, rating_in, load_sem.at[1])
            load_mask = pltpu.make_async_copy(mask_hbm, mask_in, load_sem.at[2])
            load_counts = pltpu.make_async_copy(counts_hbm, counts, load_sem.at[3])
            load_item = pltpu.make_async_copy(item_hbm, item_in.at[0], recv_sem.at[0])
            for load in (load_user, load_rating, load_mask, load_counts, load_item):
                load.start()
            barrier = pltpu.get_barrier_semaphore()
            for neighbour in (left, right):
                pl.semaphore_signal(barrier, inc=1, device_id={"shard": neighbour}, device_id_type=MESH)

            spare = GROUP * groups - LANES * blocks
            if spare:
                ut[groups - 1, :, pl.ds(GROUP - spare, spare)] = jnp.zeros((rank_dim, spare), full)
                uth[groups - 1, :, pl.ds(GROUP - spare, spare)] = jnp.zeros((rank_dim, spare), half)
                for j in range(group_size):
                    rt[j, groups - 1, :, pl.ds(GROUP - spare, spare)] = jnp.full((items_dev, spare), jnp.nan, full)
            load_user.wait()
            for b in range(blocks):
                g, s = divmod(b * LANES, GROUP)
                blk = rows_of(user_in, b).T
                ut[g, :, pl.ds(s, LANES)] = blk
                uth[g, :, pl.ds(s, LANES)] = blk.astype(half)
            load_rating.wait()
            load_mask.wait()
            for b in range(blocks):
                g, s = divmod(b * LANES, GROUP)
                blk = jnp.where(rows_of(mask_in, b) != 0, rows_of(rating_in, b), jnp.nan).T
                for j in range(group_size):
                    rt[j, g, :, pl.ds(s, LANES)] = blk[items_dev * j:items_dev * (j + 1)]
            load_counts.wait()
            pl.semaphore_wait(barrier, 2)

            def errors(item_now, col, limit):
                item_half = item_now.astype(half)
                errs = []
                for g in range(groups):
                    approx = jnp.dot(item_half, uth[g], preferred_element_type=full)
                    rating = rt[col, g]
                    errs.append(jnp.where(rating <= limit, approx - rating, 0.0).astype(half))
                return errs

            def next_item(item_now, errs, keep):
                grad = None
                for g in range(0, groups, 2):
                    both = jnp.concatenate(errs[g:g + 2], axis=0)
                    users = jnp.concatenate([uth[g], uth[g + 1]], axis=0)
                    prod = lax.dot_general(both, users, (((1,), (1,)), ((), ())), preferred_element_type=full)
                    part = prod[:items_dev, :rank_dim] + prod[items_dev:, rank_dim:]
                    grad = part if grad is None else grad + part
                return keep * item_now - step_size * grad

            def update_users(item_now, errs, keep):
                item_t = item_now.T.astype(half)
                for g in range(groups):
                    grad = jnp.dot(item_t, errs[g], preferred_element_type=full)
                    fresh = keep * ut[g] - step_size * grad
                    ut[g] = fresh
                    uth[g] = fresh.astype(half)

            def hop(t):
                return pltpu.make_async_remote_copy(
                    src_ref=item_sent.at[t], dst_ref=item_in.at[t + 1],
                    send_sem=send_sem.at[t], recv_sem=recv_sem.at[t + 1],
                    device_id={"shard": left}, device_id_type=MESH)

            def arrived(t):
                return pltpu.make_async_copy(item_in.at[t], item_in.at[t], recv_sem.at[t])

            def sub_epoch(t, carry):
                col = lax.rem(me + t, group_size)
                count = counts[0, col]
                arrived(t).wait()
                item_now = item_in[t]
                for k in range(STEPS_MAX):
                    limit = jnp.where(k < count, full(biggest), full(-jnp.inf))
                    keep = jnp.where(k < count, full(shrink), full(1.0))
                    errs = errors(item_now, col, limit)
                    item_new = next_item(item_now, errs, keep)
                    if k == STEPS_MAX - 1:
                        item_sent[t] = item_new
                        hop(t).start()
                    update_users(item_now, errs, keep)
                    item_now = item_new
                return carry

            lax.fori_loop(0, sweeps, sub_epoch, 0)
            for b in range(blocks):
                g, s = divmod(b * LANES, GROUP)
                rows = min(LANES, users_dev - LANES * b)
                user_out[pl.ds(LANES * b, rows), :] = ut[g, :, pl.ds(s, LANES)].T[:rows]
            for t in range(sweeps):
                hop(t).wait_send()
            arrived(sweeps).wait()
            item_out[...] = item_in[sweeps]

        vmem = pl.BlockSpec(memory_space=pltpu.VMEM)
        hbm = pl.BlockSpec(memory_space=pl.ANY)
        user_fin, item_fin = pl.pallas_call(
            sweep_kernel,
            out_shape=(pltpu.VMEM(user_init.shape, full), pltpu.VMEM(item_init.shape, full)),
            in_specs=[hbm] * 5,
            out_specs=(vmem, vmem),
            scratch_shapes=[
                pltpu.SMEM(step_counts.shape, jnp.int32),
                pltpu.VMEM(ratings.shape, full),
                pltpu.VMEM(obs_mask.shape, jnp.int32),
                pltpu.VMEM(user_init.shape, full),
                pltpu.VMEM((sweeps + 1,) + item_init.shape, full),
                pltpu.VMEM((sweeps,) + item_init.shape, full),
                pltpu.VMEM((group_size, groups, items_dev, GROUP), full),
                pltpu.VMEM((groups, rank_dim, GROUP), full),
                pltpu.VMEM((groups, rank_dim, GROUP), half),
                pltpu.SemaphoreType.DMA((4,)),
                pltpu.SemaphoreType.DMA((sweeps,)),
                pltpu.SemaphoreType.DMA((sweeps + 1,)),
            ],
            compiler_params=pltpu.CompilerParams(collective_id=0, has_side_effects=True),
            name="sweeps",
        )(step_counts, ratings, obs_mask, user_init, item_init)

        user_fin, item_fin = (pltpu.with_memory_space_constraint(x, pltpu.VMEM) for x in (user_fin, item_fin))

        def finish_kernel(user_ref, item_ref, user_out, item_out, sem):
            copies = [pltpu.make_async_copy(user_ref, user_out, sem.at[0]), pltpu.make_async_copy(item_ref, item_out, sem.at[1])]
            for copy in copies:
                copy.start()
            for copy in copies:
                copy.wait()

        return pl.pallas_call(
            finish_kernel,
            out_shape=(jax.ShapeDtypeStruct(user_init.shape, full), jax.ShapeDtypeStruct(item_init.shape, full)),
            in_specs=[vmem, vmem],
            out_specs=(hbm, hbm),
            scratch_shapes=[pltpu.SemaphoreType.DMA((2,))],
            name="finish",
        )(user_fin, item_fin)

    return jax.shard_map(local_run, mesh=mesh, in_specs=(row_spec,) * 5, out_specs=(row_spec, row_spec), check_vma=False)
```

time: 105 us -> 32.8 us (0.31)
  the two profiles are of different devices: /device:TPU:1 before, /device:TPU:0 now
where the time goes in v2:
time: 32.8 us; the launch traced here: 32.6 us
  Pallas kernels  32 us (98%)
  between operations  0.64 us (2%)
    pallas_call x1, Pallas kernels, local_run(): pl.pallas_call(sweep_kernel, out_shape=(pltpu.VMEM(user_init.shape, full)...  31.2 us
    pallas_call x1, Pallas kernels, local_run(): pl.pallas_call(finish_kernel, out_shape=(jax.ShapeDtypeStruct(user_init.s...  0.78 us

profile of v2, /device:TPU:0, one launch (start us, length us, event | category | flops | bytes accessed | tf_op | source)
XLA Modules:
  0.0 32.6 jit_solution(4189756860742235594)
XLA Ops:
  0.6 31.2 %sweeps.1 = (f32[864,128]{1,0:T(8,128)S(1)}, f32[32,128]{1,0:T(8,128)S(1)}) custom-call(s32[1,4]{1,0:T(1,128)} %counts_hbm.1, f32[864,128]{1,0:T(8,128)} %rating_hbm.1, s32[864,128]{1,0:T(8,128)} %mask_hbm.1, f32[864,128]{1,0:T(8,128)} %user_hbm.1, f32[32,128]{1,0:T(8,128)} %item_hbm.1), custom_call_target="tpu_custom_call" | custom-call | tf_op jit(solution)/shard_map/sweeps/pallas_call | solution.py:143
  31.9 0.8 %finish.1 = (f32[864,128]{1,0:T(8,128)}, f32[32,128]{1,0:T(8,128)}) custom-call(f32[864,128]{1,0:T(8,128)S(1)} %get-tuple-element.4.user_ref, f32[32,128]{1,0:T(8,128)S(1)} %get-tuple-element.5.item_ref), custom_call_target="tpu_custom_call" | custom-call | tf_op jit(solution)/shard_map/finish/pallas_call | solution.py:175

commit v3 on v2

--- a/solution.py
+++ b/solution.py
@@ -73,34 +73,26 @@
                 for j in range(group_size):
                     rt[j, g, :, pl.ds(s, LANES)] = blk[items_dev * j:items_dev * (j + 1)]
             load_counts.wait()
-            pl.semaphore_wait(barrier, 2)
-
-            def errors(item_now, col, limit):
-                item_half = item_now.astype(half)
-                errs = []
-                for g in range(groups):
-                    approx = jnp.dot(item_half, uth[g], preferred_element_type=full)
-                    rating = rt[col, g]
-                    errs.append(jnp.where(rating <= limit, approx - rating, 0.0).astype(half))
-                return errs
-
-            def next_item(item_now, errs, keep):
-                grad = None
-                for g in range(0, groups, 2):
-                    both = jnp.concatenate(errs[g:g + 2], axis=0)
-                    users = jnp.concatenate([uth[g], uth[g + 1]], axis=0)
-                    prod = lax.dot_general(both, users, (((1,), (1,)), ((), ())), preferred_element_type=full)
-                    part = prod[:items_dev, :rank_dim] + prod[items_dev:, rank_dim:]
-                    grad = part if grad is None else grad + part
-                return keep * item_now - step_size * grad
-
-            def update_users(item_now, errs, keep):
-                item_t = item_now.T.astype(half)
-                for g in range(groups):
-                    grad = jnp.dot(item_t, errs[g], preferred_element_type=full)
-                    fresh = keep * ut[g] - step_size * grad
-                    ut[g] = fresh
-                    uth[g] = fresh.astype(half)
+            load_item.wait()
+
+            def error(g, item_half, col, limit):
+                approx = jnp.dot(item_half, uth[g], preferred_element_type=full)
+                rating = rt[col, g]
+                return jnp.where(rating <= limit, approx - rating, 0.0).astype(half)
+
+            def grad_pair(a, b, errs):
+                both = jnp.concatenate([errs[a], errs[b]], axis=0)
+                users = jnp.concatenate([uth[a].T, uth[b].T], axis=1)
+                prod = jnp.dot(both, users, preferred_element_type=full)
+                return prod[:items_dev, :rank_dim] + prod[items_dev:, rank_dim:]
+
+            def user_grad(g, item_t, errs):
+                return jnp.dot(item_t, errs[g], preferred_element_type=full)
+
+            def update(g, grad, keep):
+                fresh = keep * ut[g] - step_size * grad
+                ut[g] = fresh
+                uth[g] = fresh.astype(half)
 
             def hop(t):
                 return pltpu.make_async_remote_copy(
@@ -111,24 +103,50 @@
             def arrived(t):
                 return pltpu.make_async_copy(item_in.at[t], item_in.at[t], recv_sem.at[t])
 
-            def sub_epoch(t, carry):
+            def sub_epoch(t, first):
                 col = lax.rem(me + t, group_size)
                 count = counts[0, col]
-                arrived(t).wait()
-                item_now = item_in[t]
+                if first:
+                    item_now = item_in[t]
+                    item_half = item_now.astype(half)
+                else:
+                    arrived(t).wait()
+                    item_now = item_in[t]
+                    item_half = item_now.astype(half)
                 for k in range(STEPS_MAX):
                     limit = jnp.where(k < count, full(biggest), full(-jnp.inf))
                     keep = jnp.where(k < count, full(shrink), full(1.0))
-                    errs = errors(item_now, col, limit)
-                    item_new = next_item(item_now, errs, keep)
+                    item_t = item_half.T
+                    errs, user_grads, parts = {}, {}, []
+                    errs[0] = error(0, item_half, col, limit)
+                    errs[1] = error(1, item_half, col, limit)
+                    errs[2] = error(2, item_half, col, limit)
+                    errs[3] = error(3, item_half, col, limit)
+                    user_grads[0] = user_grad(0, item_t, errs)
+                    parts.append(grad_pair(0, 1, errs))
+                    parts.append(grad_pair(2, 3, errs))
+                    item_now = keep * item_now - step_size * sum(parts[1:], parts[0])
+                    half_new = item_now.astype(half)
                     if k == STEPS_MAX - 1:
-                        item_sent[t] = item_new
+                        if first:
+                            pl.semaphore_wait(barrier, 2)
+                        item_sent[t] = item_now
                         hop(t).start()
-                    update_users(item_now, errs, keep)
-                    item_now = item_new
+                    user_grads[1] = user_grad(1, item_t, errs)
+                    user_grads[2] = user_grad(2, item_t, errs)
+                    user_grads[3] = user_grad(3, item_t, errs)
+                    update(0, user_grads[0], keep)
+                    update(1, user_grads[1], keep)
+                    update(2, user_grads[2], keep)
+                    update(3, user_grads[3], keep)
+                    item_half = half_new
+
+            def middle(t, carry):
+                sub_epoch(t, False)
                 return carry
 
-            lax.fori_loop(0, sweeps, sub_epoch, 0)
+            sub_epoch(0, True)
+            lax.fori_loop(1, sweeps, middle, 0)
             for b in range(blocks):
                 g, s = divmod(b * LANES, GROUP)
                 rows = min(LANES, users_dev - LANES * b)

time: 32.8 us -> 31.8 us (0.970)
  Pallas kernels: 32 us -> 31.1 us
    pallas_call x1, Pallas kernels: 31.2 us -> 30.3 us  [local_run(): pl.pallas_call(sweep_kernel, out_shape=(pltpu.VMEM(user_init.shape, full)...]
where the time goes in v3:
time: 31.8 us; the launch traced here: 31.7 us
  Pallas kernels  31.1 us (98%)
  between operations  0.64 us (2%)
    pallas_call x1, Pallas kernels, local_run(): pl.pallas_call(sweep_kernel, out_shape=(pltpu.VMEM(user_init.shape, full)...  30.3 us
    pallas_call x1, Pallas kernels, local_run(): pl.pallas_call(finish_kernel, out_shape=(jax.ShapeDtypeStruct(user_init.s...  0.78 us

profile of v3, /device:TPU:0, one launch (start us, length us, event | category | flops | bytes accessed | tf_op | source)
XLA Modules:
  0.0 31.7 jit_solution(8242414296838930178)
XLA Ops:
  0.6 30.3 %sweeps.1 = (f32[864,128]{1,0:T(8,128)S(1)}, f32[32,128]{1,0:T(8,128)S(1)}) custom-call(s32[1,4]{1,0:T(1,128)} %counts_hbm.1, f32[864,128]{1,0:T(8,128)} %rating_hbm.1, s32[864,128]{1,0:T(8,128)} %mask_hbm.1, f32[864,128]{1,0:T(8,128)} %user_hbm.1, f32[32,128]{1,0:T(8,128)} %item_hbm.1), custom_call_target="tpu_custom_call" | custom-call | tf_op jit(solution)/shard_map/sweeps/pallas_call | solution.py:161
  30.9 0.8 %finish.1 = (f32[864,128]{1,0:T(8,128)}, f32[32,128]{1,0:T(8,128)}) custom-call(f32[864,128]{1,0:T(8,128)S(1)} %get-tuple-element.4.user_ref, f32[32,128]{1,0:T(8,128)S(1)} %get-tuple-element.5.item_ref), custom_call_target="tpu_custom_call" | custom-call | tf_op jit(solution)/shard_map/finish/pallas_call | solution.py:193

commit v4 on v3

--- a/solution.py
+++ b/solution.py
@@ -55,10 +55,7 @@
 
             spare = GROUP * groups - LANES * blocks
             if spare:
-                ut[groups - 1, :, pl.ds(GROUP - spare, spare)] = jnp.zeros((rank_dim, spare), full)
                 uth[groups - 1, :, pl.ds(GROUP - spare, spare)] = jnp.zeros((rank_dim, spare), half)
-                for j in range(group_size):
-                    rt[j, groups - 1, :, pl.ds(GROUP - spare, spare)] = jnp.full((items_dev, spare), jnp.nan, full)
             load_user.wait()
             for b in range(blocks):
                 g, s = divmod(b * LANES, GROUP)
@@ -75,24 +72,29 @@
             load_counts.wait()
             load_item.wait()
 
+            def live_of(g):
+                return min(GROUP, LANES * blocks - GROUP * g)
+
             def error(g, item_half, col, limit):
-                approx = jnp.dot(item_half, uth[g], preferred_element_type=full)
-                rating = rt[col, g]
-                return jnp.where(rating <= limit, approx - rating, 0.0).astype(half)
-
-            def grad_pair(a, b, errs):
-                both = jnp.concatenate([errs[a], errs[b]], axis=0)
-                users = jnp.concatenate([uth[a].T, uth[b].T], axis=1)
-                prod = jnp.dot(both, users, preferred_element_type=full)
-                return prod[:items_dev, :rank_dim] + prod[items_dev:, rank_dim:]
+                approx = jnp.dot(item_half, uth[g, :, pl.ds(0, live_of(g))], preferred_element_type=full)
+                live = live_of(g)
+                rating = rt[col, g, :, pl.ds(0, live)]
+                err = jnp.where(rating <= limit, approx - rating, 0.0).astype(half)
+                return err
+
+            def grad_deep(gs, errs):
+                wide = jnp.concatenate([errs[g] for g in gs], axis=1)
+                users = jnp.concatenate([uth[g, :, pl.ds(0, live_of(g))].T for g in gs], axis=0)
+                return jnp.dot(wide, users, preferred_element_type=full)
 
             def user_grad(g, item_t, errs):
                 return jnp.dot(item_t, errs[g], preferred_element_type=full)
 
             def update(g, grad, keep):
-                fresh = keep * ut[g] - step_size * grad
-                ut[g] = fresh
-                uth[g] = fresh.astype(half)
+                cols = pl.ds(0, live_of(g))
+                fresh = keep * ut[g, :, cols] - step_size * grad
+                ut[g, :, cols] = fresh
+                uth[g, :, cols] = fresh.astype(half)
 
             def hop(t):
                 return pltpu.make_async_remote_copy(
@@ -118,13 +120,13 @@
                     keep = jnp.where(k < count, full(shrink), full(1.0))
                     item_t = item_half.T
                     errs, user_grads, parts = {}, {}, []
+                    errs[2] = error(2, item_half, col, limit)
                     errs[0] = error(0, item_half, col, limit)
+                    errs[3] = error(3, item_half, col, limit)
                     errs[1] = error(1, item_half, col, limit)
-                    errs[2] = error(2, item_half, col, limit)
-                    errs[3] = error(3, item_half, col, limit)
-                    user_grads[0] = user_grad(0, item_t, errs)
-                    parts.append(grad_pair(0, 1, errs))
-                    parts.append(grad_pair(2, 3, errs))
+                    parts.append(grad_deep((0, 1), errs))
+                    user_grads[2] = user_grad(2, item_t, errs)
+                    parts.append(grad_deep((2, 3), errs))
                     item_now = keep * item_now - step_size * sum(parts[1:], parts[0])
                     half_new = item_now.astype(half)
                     if k == STEPS_MAX - 1:
@@ -132,13 +134,13 @@
                             pl.semaphore_wait(barrier, 2)
                         item_sent[t] = item_now
                         hop(t).start()
+                    user_grads[0] = user_grad(0, item_t, errs)
+                    user_grads[3] = user_grad(3, item_t, errs)
                     user_grads[1] = user_grad(1, item_t, errs)
-                    user_grads[2] = user_grad(2, item_t, errs)
-                    user_grads[3] = user_grad(3, item_t, errs)
+                    update(2, user_grads[2], keep)
                     update(0, user_grads[0], keep)
+                    update(3, user_grads[3], keep)
                     update(1, user_grads[1], keep)
-                    update(2, user_grads[2], keep)
-                    update(3, user_grads[3], keep)
                     item_half = half_new
 
             def middle(t, carry):

time: 31.8 us -> 31.6 us (level)
  no operation moved by 1% of the time
where the time goes in v4:
time: 31.6 us; the launch traced here: 31.5 us
  Pallas kernels  30.8 us (97%)
  between operations  0.64 us (2%)
    pallas_call x1, Pallas kernels, local_run(): pl.pallas_call(sweep_kernel, out_shape=(pltpu.VMEM(user_init.shape, full)...  30 us
    pallas_call x1, Pallas kernels, local_run(): pl.pallas_call(finish_kernel, out_shape=(jax.ShapeDtypeStruct(user_init.s...  0.78 us

profile of v4, /device:TPU:0, one launch (start us, length us, event | category | flops | bytes accessed | tf_op | source)
XLA Modules:
  0.0 31.5 jit_solution(15771345859406682415)
XLA Ops:
  0.6 30.0 %sweeps.1 = (f32[864,128]{1,0:T(8,128)S(1)}, f32[32,128]{1,0:T(8,128)S(1)}) custom-call(s32[1,4]{1,0:T(1,128)} %counts_hbm.1, f32[864,128]{1,0:T(8,128)} %rating_hbm.1, s32[864,128]{1,0:T(8,128)} %mask_hbm.1, f32[864,128]{1,0:T(8,128)} %user_hbm.1, f32[32,128]{1,0:T(8,128)} %item_hbm.1), custom_call_target="tpu_custom_call" | custom-call | tf_op jit(solution)/shard_map/sweeps/pallas_call | solution.py:163
  30.7 0.8 %finish.1 = (f32[864,128]{1,0:T(8,128)}, f32[32,128]{1,0:T(8,128)}) custom-call(f32[864,128]{1,0:T(8,128)S(1)} %get-tuple-element.4.user_ref, f32[32,128]{1,0:T(8,128)S(1)} %get-tuple-element.5.item_ref), custom_call_target="tpu_custom_call" | custom-call | tf_op jit(solution)/shard_map/finish/pallas_call | solution.py:195
